TPU v7x, 128 devices: a whole 4x4x4 slice. The times are simulated.
128 devices in a mesh: dev: 128 (over x, y, z, core).
Axes of the slice: x: 4, y: 4, z: 4, core: 2. Of those that a mesh axis runs over, the one named last changes fastest.
Arguments:
- source: bfloat16 [48, 1048576], P(None, 'dev'), may hold values from -6 to 6
- weights: bfloat16 [81920, 128, 128], P('dev'), may hold values from -0.01953125 to 0.01953125
- tile_map: int32 [3, 81920], P(None, 'dev'), may hold values from 0 to 127, as said below
- tile_count: int32 [128], P('dev'), may hold values from 160 to 640, as said below
Outputs:
- acoustic_source: float32 [48, 16384], P(None, 'dev')
Inputs may be any that keep to these rules, and one draw needn't show every extreme that they name: `tile_map`: row 0 is a CFD block of the owning device; row 2 an acoustic block of the destination. Row 1 is a device at cyclic distance at most 4 from the owner in device order, or at distance exactly 128 // 2 (counted upward); every device has used slots at distance +4, -4 and 128 // 2. `tile_count`: some device uses all its slots.
All inputs are finite; a program needn't handle non-finite values.
Results may differ from a plain program's by a relative error of at most 0.0003.
Values sent between devices are 32-bit elements; how exact they have to be, the bound alone decides.
A program may use at most 128 MiB of HBM per device.

v0:
```python
import jax
import jax.numpy as jnp
from jax import lax
from jax.sharding import PartitionSpec as P

REACH = 4
ACU_BLK_DEV = 1


def passed_along(value, axis, steps):
    count = lax.axis_size(axis)
    pairs = [(source, (source + steps) % count) for source in range(count)]
    return lax.ppermute(value, axis, pairs)


def on_device(source, weights, tile_map, tile_count):
    feat, cells = source.shape
    tiles, blk_size = (weights.shape[0], weights.shape[1])
    acu = ACU_BLK_DEV
    blocks = source.reshape(feat, cells // blk_size, blk_size)
    picked = jnp.take(blocks, tile_map[0], axis=1)
    products = jnp.einsum("ftc,tcn->tfn", picked, weights, preferred_element_type=jnp.float32)
    used = jnp.arange(tiles, dtype=jnp.int32) < tile_count[0]
    products = jnp.where(used[:, None, None], products, 0.0)
    devices = lax.axis_size("dev")
    own = lax.axis_index("dev")
    half_way = devices // 2
    upward = (tile_map[1] - own) % devices
    distance = jnp.where(upward > half_way, upward - devices, upward)
    far_slot = 2 * REACH + 1
    is_far = jnp.logical_and(upward == half_way, half_way > REACH)
    slot_key = jnp.where(is_far, far_slot, distance + REACH)
    segment_key = slot_key * acu + tile_map[2]
    outgoing = jax.ops.segment_sum(products, segment_key, num_segments=(2 * REACH + 2) * acu)
    outgoing = outgoing.reshape(2 * REACH + 2, acu, feat, blk_size)
    total = outgoing[REACH]
    for index in range(2 * REACH + 1):
        if index != REACH:
            total = total + passed_along(outgoing[index], "dev", index - REACH)
    total = total + passed_along(outgoing[far_slot], "dev", half_way)
    return jnp.transpose(total, (1, 0, 2)).reshape(feat, acu * blk_size)


def solution(mesh):
    return jax.shard_map(
        on_device,
        mesh=mesh,
        in_specs=(P(None, "dev"), P("dev", None, None), P(None, "dev"), P("dev")),
        out_specs=P(None, "dev"),
        check_vma=False,
    )
```

profile of v0, /device:TPU:1, one launch (start us, length us, event | category | flops | bytes accessed | tf_op | source)
XLA Modules:
  0.0 110.8 jit_solution(4363870252319548078)
XLA Ops:
  0.0 0.8 slice_reduce_fusion
  0.8 0.9 fusion.13
  1.7 0.1 copy_bitcast_fusion
  2.5 4.8 %gather_fusion = bf16[640,48,128]{2,1,0:T(8,128)(2,1)} fusion(bf16[48,64,128]{2,0,1:T(8,128)(2,1)S(1)} %copy_bitcast_fusion, s32[1024]{0:T(1024)S(1)} %pad_clamp_fusion), kind=kCustom, calls=%fused_computation | custom fusion | bytes 15731200 | tf_op jit(solution)/shard_map/jit(_take)/gather | solution.py:21
  7.2 16.4 %convolution_select_fusion = f32[640,48,128]{2,1,0:T(8,128)} fusion(bf16[640,128,128]{2,1,0:T(8,128)(2,1)} %param.5, bf16[640,48,128]{2,1,0:T(8,128)(2,1)} %gather_fusion, pred[640]{0:T(1024)(128)(4,1)S(1)} %get-tuple-element.17, pred[640]{0:T(1024)(128)(4,1)S(1)} %get-tuple-element.16), kind=kOutput, calls=%fused_computation.2 | convolution fusion | flops 1014497280 | bytes 44565760 | tf_op jit(solution)/shard_map/ftc,tcn->tfn/dot_general | solution.py:22
  23.6 62.2 %scatter_fusion = f32[10,48,128]{2,1,0:T(8,128)S(1)} fusion(f32[10,48,128]{2,1,0:T(8,128)S(1)} %broadcast_in_dim.31, s32[640]{0:T(1024)S(1)} %get-tuple-element.6, f32[640,48,128]{2,1,0:T(8,128)} %convolution_select_fusion), kind=kCustom, calls=%fused_computation.1 | custom fusion | flops 3932160 | bytes 47188480 | tf_op jit(solution)/shard_map/scatter-add | solution.py:34
  85.9 9.1 %collective-permute-start = (f32[1,48,128]{2,1,0:T(8,128)S(1)}, f32[1,48,128]{2,1,0:T(8,128)S(1)}, u32[]{:S(2)}, u32[]{:S(2)}) collective-permute-start(f32[1,48,128]{2,1,0:T(8,128)S(1)} %get-tuple-element.7), channel_id=1, source_target_pairs={{0,124},{1,125},{2,126},{3,127},{4,0},{5,1},{6,2},{7,3},{8,4},{9,5... | collective-permute-start | bytes 73736 | tf_op jit(solution)/shard_map/ppermute | solution.py:13
  95.0 1.3 %collective-permute-start.1 = (f32[1,48,128]{2,1,0:T(8,128)S(1)}, f32[1,48,128]{2,1,0:T(8,128)S(1)}, u32[]{:S(2)}, u32[]{:S(2)}) collective-permute-start(f32[1,48,128]{2,1,0:T(8,128)S(1)} %get-tuple-element.15), channel_id=1, source_target_pairs={{0,125},{1,126},{2,127},{3,0},{4,1},{5,2},{6,3},{7,4},{8,5},{9,6},... | collective-permute-start | bytes 73736 | tf_op jit(solution)/shard_map/ppermute | solution.py:13
  96.3 0.0 collective-permute-start.2
  96.3 2.7 %collective-permute-start.3 = (f32[1,48,128]{2,1,0:T(8,128)S(1)}, f32[1,48,128]{2,1,0:T(8,128)S(1)}, u32[]{:S(2)}, u32[]{:S(2)}) collective-permute-start(f32[1,48,128]{2,1,0:T(8,128)S(1)} %get-tuple-element.13), channel_id=1, source_target_pairs={{0,127},{1,0},{2,1},{3,2},{4,3},{5,4},{6,5},{7,6},{8,7},{9,8},{10,... | collective-permute-start | bytes 73736 | tf_op jit(solution)/shard_map/ppermute | solution.py:13
  99.0 0.0 collective-permute-start.4
  99.0 0.0 collective-permute-done
  99.0 0.5 collective-permute-start.5
  99.5 0.3 collective-permute-done.1
  99.8 1.3 %collective-permute-start.6 = (f32[1,48,128]{2,1,0:T(8,128)S(1)}, f32[1,48,128]{2,1,0:T(8,128)S(1)}, u32[]{:S(2)}, u32[]{:S(2)}) collective-permute-start(f32[1,48,128]{2,1,0:T(8,128)S(1)} %get-tuple-element.10), channel_id=1, source_target_pairs={{0,3},{1,4},{2,5},{3,6},{4,7},{5,8},{6,9},{7,10},{8,11},{9,12},{10... | collective-permute-start | bytes 73736 | tf_op jit(solution)/shard_map/ppermute | solution.py:13
  101.1 0.0 collective-permute-done.2
  101.1 2.6 %collective-permute-start.7 = (f32[1,48,128]{2,1,0:T(8,128)S(1)}, f32[1,48,128]{2,1,0:T(8,128)S(1)}, u32[]{:S(2)}, u32[]{:S(2)}) collective-permute-start(f32[1,48,128]{2,1,0:T(8,128)S(1)} %get-tuple-element.9), channel_id=1, source_target_pairs={{0,4},{1,5},{2,6},{3,7},{4,8},{5,9},{6,10},{7,11},{8,12},{9,13},{1... | collective-permute-start | bytes 73736 | tf_op jit(solution)/shard_map/ppermute | solution.py:13
  103.8 0.0 collective-permute-done.3
  103.8 0.5 collective-permute-start.8
  104.3 0.0 collective-permute-done.4
  104.3 3.2 %collective-permute-done.5 = f32[1,48,128]{2,1,0:T(8,128)S(1)} collective-permute-done((f32[1,48,128]{2,1,0:T(8,128)S(1)}, f32[1,48,128]{2,1,0:T(8,128)S(1)}, u32[]{:S(2)}, u32[]{:S(2)}) %collective-permute-start.5) | collective-permute-done | bytes 24608 | tf_op jit(solution)/shard_map/ppermute | solution.py:13
  107.5 1.2 %collective-permute-done.6 = f32[1,48,128]{2,1,0:T(8,128)S(1)} collective-permute-done((f32[1,48,128]{2,1,0:T(8,128)S(1)}, f32[1,48,128]{2,1,0:T(8,128)S(1)}, u32[]{:S(2)}, u32[]{:S(2)}) %collective-permute-start.6) | collective-permute-done | bytes 24608 | tf_op jit(solution)/shard_map/ppermute | solution.py:13
  108.7 1.4 %collective-permute-done.7 = f32[1,48,128]{2,1,0:T(8,128)S(1)} collective-permute-done((f32[1,48,128]{2,1,0:T(8,128)S(1)}, f32[1,48,128]{2,1,0:T(8,128)S(1)}, u32[]{:S(2)}, u32[]{:S(2)}) %collective-permute-start.7) | collective-permute-done | bytes 24608 | tf_op jit(solution)/shard_map/ppermute | solution.py:13
  110.2 0.6 fusion.12
  (7 shorter events, 0.1 us)
Async XLA Ops:
  0.0 1.7 %copy-start = (bf16[48,8192]{1,0:T(8,128)(2,1)S(1)}, bf16[48,8192]{1,0:T(8,128)(2,1)}, u32[]{:S(2)}) copy-start(bf16[48,8192]{1,0:T(8,128)(2,1)} %param.4) | copy-start | bytes 2359300
  85.9 13.1 %collective-permute-start = (f32[1,48,128]{2,1,0:T(8,128)S(1)}, f32[1,48,128]{2,1,0:T(8,128)S(1)}, u32[]{:S(2)}, u32[]{:S(2)}) collective-permute-start(f32[1,48,128]{2,1,0:T(8,128)S(1)} %get-tuple-element.7), channel_id=1, source_target_pairs={{0,124},{1,125},{2,126},{3,127},{4,0},{5,1},{6,2},{7,3},{8,4},{9,5... | collective-permute-start | bytes 73736 | tf_op jit(solution)/shard_map/ppermute | solution.py:13
  95.0 4.8 %collective-permute-start.1 = (f32[1,48,128]{2,1,0:T(8,128)S(1)}, f32[1,48,128]{2,1,0:T(8,128)S(1)}, u32[]{:S(2)}, u32[]{:S(2)}) collective-permute-start(f32[1,48,128]{2,1,0:T(8,128)S(1)} %get-tuple-element.15), channel_id=1, source_target_pairs={{0,125},{1,126},{2,127},{3,0},{4,1},{5,2},{6,3},{7,4},{8,5},{9,6},... | collective-permute-start | bytes 73736 | tf_op jit(solution)/shard_map/ppermute | solution.py:13
  96.3 4.8 %collective-permute-start.2 = (f32[1,48,128]{2,1,0:T(8,128)S(1)}, f32[1,48,128]{2,1,0:T(8,128)S(1)}, u32[]{:S(2)}, u32[]{:S(2)}) collective-permute-start(f32[1,48,128]{2,1,0:T(8,128)S(1)} %get-tuple-element.14), channel_id=1, source_target_pairs={{0,126},{1,127},{2,0},{3,1},{4,2},{5,3},{6,4},{7,5},{8,6},{9,7},{1... | collective-permute-start | bytes 73736 | tf_op jit(solution)/shard_map/ppermute | solution.py:13
  96.3 7.5 %collective-permute-start.3 = (f32[1,48,128]{2,1,0:T(8,128)S(1)}, f32[1,48,128]{2,1,0:T(8,128)S(1)}, u32[]{:S(2)}, u32[]{:S(2)}) collective-permute-start(f32[1,48,128]{2,1,0:T(8,128)S(1)} %get-tuple-element.13), channel_id=1, source_target_pairs={{0,127},{1,0},{2,1},{3,2},{4,3},{5,4},{6,5},{7,6},{8,7},{9,8},{10,... | collective-permute-start | bytes 73736 | tf_op jit(solution)/shard_map/ppermute | solution.py:13
  99.0 5.3 %collective-permute-start.4 = (f32[1,48,128]{2,1,0:T(8,128)S(1)}, f32[1,48,128]{2,1,0:T(8,128)S(1)}, u32[]{:S(2)}, u32[]{:S(2)}) collective-permute-start(f32[1,48,128]{2,1,0:T(8,128)S(1)} %get-tuple-element.12), channel_id=1, source_target_pairs={{0,1},{1,2},{2,3},{3,4},{4,5},{5,6},{6,7},{7,8},{8,9},{9,10},{10,1... | collective-permute-start | bytes 73736 | tf_op jit(solution)/shard_map/ppermute | solution.py:13
  99.0 8.5 %collective-permute-start.5 = (f32[1,48,128]{2,1,0:T(8,128)S(1)}, f32[1,48,128]{2,1,0:T(8,128)S(1)}, u32[]{:S(2)}, u32[]{:S(2)}) collective-permute-start(f32[1,48,128]{2,1,0:T(8,128)S(1)} %get-tuple-element.11), channel_id=1, source_target_pairs={{0,2},{1,3},{2,4},{3,5},{4,6},{5,7},{6,8},{7,9},{8,10},{9,11},{10,... | collective-permute-start | bytes 73736 | tf_op jit(solution)/shard_map/ppermute | solution.py:13
  99.8 8.9 %collective-permute-start.6 = (f32[1,48,128]{2,1,0:T(8,128)S(1)}, f32[1,48,128]{2,1,0:T(8,128)S(1)}, u32[]{:S(2)}, u32[]{:S(2)}) collective-permute-start(f32[1,48,128]{2,1,0:T(8,128)S(1)} %get-tuple-element.10), channel_id=1, source_target_pairs={{0,3},{1,4},{2,5},{3,6},{4,7},{5,8},{6,9},{7,10},{8,11},{9,12},{10... | collective-permute-start | bytes 73736 | tf_op jit(solution)/shard_map/ppermute | solution.py:13
  101.1 9.1 %collective-permute-start.7 = (f32[1,48,128]{2,1,0:T(8,128)S(1)}, f32[1,48,128]{2,1,0:T(8,128)S(1)}, u32[]{:S(2)}, u32[]{:S(2)}) collective-permute-start(f32[1,48,128]{2,1,0:T(8,128)S(1)} %get-tuple-element.9), channel_id=1, source_target_pairs={{0,4},{1,5},{2,6},{3,7},{4,8},{5,9},{6,10},{7,11},{8,12},{9,13},{1... | collective-permute-start | bytes 73736 | tf_op jit(solution)/shard_map/ppermute | solution.py:13
  103.8 6.4 %collective-permute-start.8 = (f32[1,48,128]{2,1,0:T(8,128)S(1)}, f32[1,48,128]{2,1,0:T(8,128)S(1)}, u32[]{:S(2)}, u32[]{:S(2)}) collective-permute-start(f32[1,48,128]{2,1,0:T(8,128)S(1)} %get-tuple-element.8), channel_id=1, source_target_pairs={{0,64},{1,65},{2,66},{3,67},{4,68},{5,69},{6,70},{7,71},{8,72},{9,... | collective-permute-start | bytes 73736 | tf_op jit(solution)/shard_map/ppermute | solution.py:13
where the time goes:
time: 113 us; the launch traced here: 111 us
  other arithmetic  63.7 us (56%)
  starting transfers between devices  18.1 us (16%)
  matrix products  16.4 us (15%)
  waiting for transfers between devices  6.17 us (5%)
  local copies, waits for them, and re-layouts  5.74 us (5%)
    scatter-add x1, other arithmetic, on_device(): jax.ops.segment_sum(products, segment_key, num_segments=(2 * REACH + 2) *...  62.2 us
    ppermute x9, starting transfers between devices, passed_along(): return lax.ppermute(value, axis, pairs)  18.1 us
    dot_general x1, matrix products, on_device(): jnp.einsum('ftc,tcn->tfn', picked, weights, preferred_element_type=jnp.fl...  16.4 us
    ppermute x9, waiting for transfers between devices, passed_along(): return lax.ppermute(value, axis, pairs)  6.17 us
    gather x1, local copies, waits for them, and re-layouts, on_device(): picked = jnp.take(blocks, tile_map[0], axis=1)  4.78 us
  transfers between devices with their start and end apart: 9, of which 4 were waited for; matrix products, arithmetic and copies ran while one was open for 0% of the time, Pallas kernels for 0%

commit v1 on v0

v1 whole, which is shorter than its diff:
```python
import functools

import jax
import jax.numpy as jnp
from jax import lax
from jax.experimental import pallas as pl
from jax.experimental.pallas import tpu as pltpu
from jax.sharding import PartitionSpec as P

REACH = 4
LANES = 128
CHUNK = 64


def kernel(n, src_hbm, w_hbm, map_hbm, cnt_hbm, out_ref, w, src, log, map_v, map_s, cnt_s, idx_v, idx_s, send, recv,
           w_sem, in_sem, send_sem, recv_sem):
    tiles, blk = w.shape[0], w.shape[1]
    feat = src.shape[1]
    chunks = tiles // CHUNK
    groups = tiles // LANES
    own = lax.axis_index("dev")
    offsets = [d for d in range(-REACH, REACH + 1) if d != 0] + [n // 2]
    partners = [lax.rem(own + (d + n), n) for d in offsets]

    map_copy = pltpu.make_async_copy(map_hbm, map_v, in_sem.at[0])
    cnt_copy = pltpu.make_async_copy(cnt_hbm, cnt_s, in_sem.at[1])
    map_copy_s = pltpu.make_async_copy(map_hbm, map_s, in_sem.at[2])
    src_copy = pltpu.make_async_copy(src, src, in_sem.at[3])
    map_copy.start()
    cnt_copy.start()
    map_copy_s.start()

    @pl.loop(0, src.shape[0])
    def _(b):
        part = pl.ds(pl.multiple_of(b * blk, blk), blk)
        pltpu.make_async_copy(src_hbm.at[:, part], src.at[b], in_sem.at[3]).start()

    def w_copy(c):
        part = pl.ds(pl.multiple_of(c * CHUNK, CHUNK), CHUNK)
        return pltpu.make_async_copy(w_hbm.at[part], w.at[part], w_sem.at[c])

    @pl.loop(0, chunks)
    def _(c):
        w_copy(c).start()

    barrier = pltpu.get_barrier_semaphore()
    for partner in partners:
        pl.semaphore_signal(barrier, inc=1, device_id=(partner,), device_id_type=pl.DeviceIdType.MESH)

    map_copy.wait()
    cnt_copy.wait()
    lane = lax.broadcasted_iota(jnp.int32, (1, LANES), 1)
    row = lax.broadcasted_iota(jnp.int32, (LANES, LANES), 0)
    keys, columns = [], []
    for g in range(groups):
        up = map_v[1:2, g * LANES:(g + 1) * LANES] - own
        up = jnp.where(up < 0, up + n, up)
        key = jnp.where(up == n // 2, 2 * REACH + 1, jnp.where(up > n // 2, up - n, up) + REACH)
        key = jnp.where(lane + g * LANES < cnt_s[0], key, 2 * REACH + 2)
        keys.append(key)
        columns.append(jnp.transpose(jnp.broadcast_to(key, (LANES, LANES))))
    last = jnp.zeros((LANES, LANES), jnp.int32)
    for g in range(groups):
        prev = jnp.zeros((LANES, LANES), jnp.int32)
        for h in range(g):
            prev = jnp.where(columns[h] == keys[g], row + (h * LANES + 1), prev)
        here = jnp.logical_and(columns[g] == keys[g], row < lane)
        prev = jnp.where(here, row + (g * LANES + 1), prev)
        idx_v[g:g + 1, :] = jnp.max(prev, axis=0, keepdims=True)
        last = jnp.where(columns[g] == lane, row + (g * LANES + 1), last)
    idx_v[groups:groups + 1, :] = jnp.max(last, axis=0, keepdims=True)
    idx_copy = pltpu.make_async_copy(idx_v, idx_s, in_sem.at[4])
    idx_copy.start()
    log[0] = jnp.zeros((feat, blk), jnp.float32)
    map_copy_s.wait()
    src_copy.wait()
    idx_copy.wait()

    @pl.loop(0, chunks)
    def _(c):
        w_copy(c).wait()
        base = c * CHUNK
        group, rest = base // LANES, lax.rem(base, LANES)
        for u in range(0, CHUNK, 2):
            blocks = [map_s[0, base + u + v] for v in range(2)]
            lhs = jnp.concatenate(
                [src[b] for b in blocks], axis=0)
            rhs = jnp.concatenate([w[base + u], w[base + u + 1]], axis=1)
            both = jnp.dot(lhs, rhs, preferred_element_type=jnp.float32)
            for v in range(2):
                product = both[v * feat:(v + 1) * feat, v * blk:(v + 1) * blk]
                log[base + u + v + 1] = product + log[idx_s[group, rest + u + v]]

    for k in range(len(offsets)):
        slot = k if k < REACH else k + 1
        send[k] = log[idx_s[groups, slot]]
    pl.semaphore_wait(barrier, len(offsets))
    copies = []
    for k, partner in enumerate(partners):
        copies.append(pltpu.make_async_remote_copy(
            src_ref=send.at[k], dst_ref=recv.at[k], send_sem=send_sem.at[k], recv_sem=recv_sem.at[k],
            device_id=(partner,), device_id_type=pl.DeviceIdType.MESH))
        copies[-1].start()
    total = log[idx_s[groups, REACH]]
    for k in range(len(offsets)):
        copies[k].wait_recv()
        total = total + recv[k]
    out_ref[...] = total
    for k in range(len(offsets)):
        copies[k].wait_send()


def on_device(source, weights, tile_map, tile_count):
    n = lax.axis_size("dev")
    feat, cells = source.shape
    tiles, blk, _ = weights.shape
    partners = 2 * REACH + 1
    groups = tiles // LANES

    return pl.pallas_call(
        functools.partial(kernel, n),
        out_shape=jax.ShapeDtypeStruct((feat, blk), jnp.float32),
        in_specs=[pl.BlockSpec(memory_space=pl.ANY)] * 4,
        out_specs=pl.BlockSpec(memory_space=pltpu.VMEM),
        scratch_shapes=[
            pltpu.VMEM((tiles, blk, blk), jnp.bfloat16),
            pltpu.VMEM((cells // blk, feat, blk), jnp.bfloat16),
            pltpu.VMEM((tiles + 1, feat, blk), jnp.float32),
            pltpu.VMEM(tile_map.shape, jnp.int32),
            pltpu.SMEM(tile_map.shape, jnp.int32),
            pltpu.SMEM((1,), jnp.int32),
            pltpu.VMEM((8, LANES), jnp.int32),
            pltpu.SMEM((8, LANES), jnp.int32),
            pltpu.VMEM((partners, feat, blk), jnp.float32),
            pltpu.VMEM((partners, feat, blk), jnp.float32),
            pltpu.SemaphoreType.DMA((tiles // CHUNK,)),
            pltpu.SemaphoreType.DMA((5,)),
            pltpu.SemaphoreType.DMA((partners,)),
            pltpu.SemaphoreType.DMA((partners,)),
        ],
        compiler_params=pltpu.CompilerParams(
            collective_id=0, has_side_effects=True, vmem_limit_bytes=67043328),
        cost_estimate=pl.CostEstimate(
            flops=2 * tiles * feat * blk * blk, bytes_accessed=tiles * blk * blk * 2, transcendentals=0),
    )(source, weights, tile_map, tile_count)


def solution(mesh):
    return jax.shard_map(
        on_device,
        mesh=mesh,
        in_specs=(P(None, "dev"), P("dev", None, None), P(None, "dev"), P("dev")),
        out_specs=P(None, "dev"),
        check_vma=False,
    )
```

time: 113 us -> 24.4 us (0.22); the launches traced: 111 us -> 24.1 us
  other arithmetic: 63.7 us -> 0 us
  Pallas kernels: 0 us -> 22.1 us
  starting transfers between devices: 18.1 us -> 0 us
  matrix products: 16.4 us -> 0 us
  waiting for transfers between devices: 6.17 us -> 0 us
  local copies, waits for them, and re-layouts: 5.74 us -> 1.35 us
    scatter-add x1 -> x0, other arithmetic: 62.2 us -> none  [on_device(): jax.ops.segment_sum(products, segment_key, num_segments=(2 * REACH + 2) *...]
    pallas_call x0 -> x1, Pallas kernels: none -> 22.1 us  [on_device(): pl.pallas_call(functools.partial(kernel, n), out_shape=jax.ShapeDtypeStru...]
    ppermute x9 -> x0, starting transfers between devices: 18.1 us -> none  [passed_along(): return lax.ppermute(value, axis, pairs)]
    dot_general x1 -> x0, matrix products: 16.4 us -> none  [on_device(): jnp.einsum('ftc,tcn->tfn', picked, weights, preferred_element_type=jnp.fl...]
    ppermute x9 -> x0, waiting for transfers between devices: 6.17 us -> none  [passed_along(): return lax.ppermute(value, axis, pairs)]
    gather x1 -> x0, local copies, waits for them, and re-layouts: 4.78 us -> none  [on_device(): picked = jnp.take(blocks, tile_map[0], axis=1)]
    unnamed x2 -> x1, local copies, waits for them, and re-layouts: 0.01 us -> 1.35 us
  transfers between devices with their start and end apart: 9 -> 0, of which waited for: 4 -> 0; matrix products, arithmetic and copies ran while one was open for 0% -> 0% of each run, Pallas kernels for 0% -> 0%
where the time goes in v1:
time: 24.4 us; the launch traced here: 24.1 us
  Pallas kernels  22.1 us (91%)
  local copies, waits for them, and re-layouts  1.35 us (6%)
  between operations  0.66 us (3%)
    pallas_call x1, Pallas kernels, on_device(): pl.pallas_call(functools.partial(kernel, n), out_shape=jax.ShapeDtypeStru...  22.1 us
    unnamed x1, local copies, waits for them, and re-layouts  1.35 us

profile of v1, /device:TPU:1, one launch (start us, length us, event | category | flops | bytes accessed | tf_op | source)
XLA Modules:
  0.0 24.1 jit_solution(3727706000546502137)
XLA Ops:
  0.7 22.1 %shard_map.46 = f32[48,128]{1,0:T(8,128)} custom-call(bf16[48,8192]{1,0:T(8,128)(2,1)} %src_hbm.1, bf16[640,128,128]{2,1,0:T(8,128)(2,1)} %w_hbm.1, s32[3,640]{1,0:T(4,128)} %map_hbm.1, s32[1]{0:T(128)S(6)} %copy.6.cnt_hbm), custom_call_target="tpu_custom_call" | custom-call | flops 1006632960 | bytes 20971520 | tf_op jit(solution)/shard_map/pallas_call | solution.py:120
  22.8 1.3 %copy.7 = f32[48,128]{1,0:T(8,128)} copy(f32[48,128]{1,0:T(8,128)} %shard_map.46) | data formatting | bytes 49152

commit v2 on v1

v2 whole, which is shorter than its diff:
```python
import functools

import jax
import jax.numpy as jnp
from jax import lax
from jax.experimental import pallas as pl
from jax.experimental.pallas import tpu as pltpu
from jax.sharding import PartitionSpec as P

REACH = 4
LANES = 128
CHUNK = 64


def kernel(n, src_hbm, w_hbm, map_hbm, cnt_s, out_ref, w, src, log, map_v, map_s, idx_v, idx_s, send, recv,
           w_sem, in_sem, send_sem, recv_sem):
    tiles, blk = w.shape[0], w.shape[1]
    feat = src.shape[1]
    chunks = tiles // CHUNK
    groups = tiles // LANES
    own = lax.axis_index("dev")
    offsets = [d for d in range(-REACH, REACH + 1) if d != 0] + [n // 2]
    partners = [lax.rem(own + (d + n), n) for d in offsets]

    map_copy = pltpu.make_async_copy(map_hbm, map_v, in_sem.at[0])
    map_copy_s = pltpu.make_async_copy(map_hbm, map_s, in_sem.at[1])
    src_copy = pltpu.make_async_copy(src, src, in_sem.at[2])
    map_copy.start()
    map_copy_s.start()

    @pl.loop(0, src.shape[0])
    def _(b):
        part = pl.ds(pl.multiple_of(b * blk, blk), blk)
        pltpu.make_async_copy(src_hbm.at[:, part], src.at[b], in_sem.at[2]).start()

    def w_copy(c):
        part = pl.ds(pl.multiple_of(c * CHUNK, CHUNK), CHUNK)
        return pltpu.make_async_copy(w_hbm.at[part], w.at[part], w_sem.at[c])

    @pl.loop(0, chunks)
    def _(c):
        w_copy(c).start()

    barrier = pltpu.get_barrier_semaphore()
    for partner in partners:
        pl.semaphore_signal(barrier, inc=1, device_id=(partner,), device_id_type=pl.DeviceIdType.MESH)

    map_copy.wait()
    lane = lax.broadcasted_iota(jnp.int32, (1, LANES), 1)
    row = lax.broadcasted_iota(jnp.int32, (LANES, LANES), 0)
    keys, columns = [], []
    for g in range(groups):
        up = map_v[1:2, g * LANES:(g + 1) * LANES] - own
        up = jnp.where(up < 0, up + n, up)
        key = jnp.where(up == n // 2, 2 * REACH + 1, jnp.where(up > n // 2, up - n, up) + REACH)
        key = jnp.where(lane + g * LANES < cnt_s[0], key, 2 * REACH + 2)
        keys.append(key)
        columns.append(jnp.transpose(jnp.broadcast_to(key, (LANES, LANES))))
    last = jnp.zeros((LANES, LANES), jnp.int32)
    for g in range(groups):
        prev = jnp.zeros((LANES, LANES), jnp.int32)
        for h in range(g):
            prev = jnp.where(columns[h] == keys[g], row + (h * LANES + 1), prev)
        here = jnp.logical_and(columns[g] == keys[g], row < lane)
        prev = jnp.where(here, row + (g * LANES + 1), prev)
        idx_v[:, g * LANES:(g + 1) * LANES] = jnp.max(prev, axis=0, keepdims=True)
        last = jnp.where(columns[g] == lane, row + (g * LANES + 1), last)
    idx_v[:, tiles:tiles + LANES] = jnp.max(last, axis=0, keepdims=True)
    idx_copy = pltpu.make_async_copy(idx_v, idx_s, in_sem.at[3])
    idx_copy.start()
    log[0] = jnp.zeros((feat, blk), jnp.float32)
    map_copy_s.wait()
    src_copy.wait()
    idx_copy.wait()

    @pl.loop(0, chunks)
    def _(c):
        w_copy(c).wait()
        base = c * CHUNK
        for u in range(0, CHUNK, 2):
            blocks = [map_s[0, base + u + v] for v in range(2)]
            lhs = jnp.concatenate(
                [src[b] for b in blocks], axis=0)
            rhs = jnp.concatenate([w[base + u], w[base + u + 1]], axis=1)
            both = jnp.dot(lhs, rhs, preferred_element_type=jnp.float32)
            for v in range(2):
                product = both[v * feat:(v + 1) * feat, v * blk:(v + 1) * blk]
                log[base + u + v + 1] = product + log[idx_s[0, base + u + v]]

    for k in range(len(offsets)):
        slot = k if k < REACH else k + 1
        send[k] = log[idx_s[0, tiles + slot]]
    pl.semaphore_wait(barrier, len(offsets))
    def transfer(k, partner):
        return pltpu.make_async_remote_copy(
            src_ref=send.at[k], dst_ref=recv.at[k], send_sem=send_sem.at[k], recv_sem=recv_sem.at[k],
            device_id=(partner,), device_id_type=pl.DeviceIdType.MESH)

    place = lax.rem(own, 4)
    for turn in range(REACH):
        step = jnp.where(place == 3, (2, 1, 4, 3)[turn], jnp.where(place == 2, (3, 2, 4, 1)[turn], REACH - turn))
        transfer(step + (REACH - 1), lax.rem(own + step, n)).start()
    for k in range(REACH):
        transfer(k, partners[k]).start()
    transfer(2 * REACH, partners[2 * REACH]).start()
    total = log[idx_s[0, tiles + REACH]]
    for k in range(len(offsets)):
        transfer(k, partners[k]).wait_recv()
        total = total + recv[k]
    out_ref[...] = total
    for k in range(len(offsets)):
        transfer(k, partners[k]).wait_send()


def on_device(source, weights, tile_map, tile_count):
    n = lax.axis_size("dev")
    feat, cells = source.shape
    tiles, blk, _ = weights.shape
    partners = 2 * REACH + 1
    hbm = [pltpu.with_memory_space_constraint(x, pltpu.HBM) for x in (source, weights, tile_map)]

    return pl.pallas_call(
        functools.partial(kernel, n),
        out_shape=pltpu.VMEM((feat, blk), jnp.float32),
        in_specs=[pl.BlockSpec(memory_space=pltpu.HBM)] * 3 + [pl.BlockSpec(memory_space=pltpu.SMEM)],
        out_specs=pl.BlockSpec(memory_space=pltpu.VMEM),
        scratch_shapes=[
            pltpu.VMEM((tiles, blk, blk), jnp.bfloat16),
            pltpu.VMEM((cells // blk, feat, blk), jnp.bfloat16),
            pltpu.VMEM((tiles + 1, feat, blk), jnp.float32),
            pltpu.VMEM(tile_map.shape, jnp.int32),
            pltpu.SMEM(tile_map.shape, jnp.int32),
            pltpu.VMEM((1, tiles + LANES), jnp.int32),
            pltpu.SMEM((1, tiles + LANES), jnp.int32),
            pltpu.VMEM((partners, feat, blk), jnp.float32),
            pltpu.VMEM((partners, feat, blk), jnp.float32),
            pltpu.SemaphoreType.DMA((tiles // CHUNK,)),
            pltpu.SemaphoreType.DMA((4,)),
            pltpu.SemaphoreType.DMA((partners,)),
            pltpu.SemaphoreType.DMA((partners,)),
        ],
        compiler_params=pltpu.CompilerParams(
            collective_id=0, has_side_effects=True, vmem_limit_bytes=48 * 1024 * 1024),
        cost_estimate=pl.CostEstimate(
            flops=2 * tiles * feat * blk * blk, bytes_accessed=tiles * blk * blk * 2, transcendentals=0),
    )(*hbm, tile_count)


def solution(mesh):
    return jax.shard_map(
        on_device,
        mesh=mesh,
        in_specs=(P(None, "dev"), P("dev", None, None), P(None, "dev"), P("dev")),
        out_specs=P(None, "dev"),
        check_vma=False,
    )
```

time: 24.4 us -> 22.1 us (0.906)
  Pallas kernels: 22.1 us -> 20.6 us
  local copies, waits for them, and re-layouts: 1.35 us -> 0.61 us
    pallas_call x1, Pallas kernels: 22.1 us -> 20.6 us  [on_device(): pl.pallas_call(functools.partial(kernel, n), out_shape=pltpu.VMEM((feat,...]
    unnamed x1, local copies, waits for them, and re-layouts: 1.35 us -> 0.61 us
where the time goes in v2:
time: 22.1 us; the launch traced here: 21.9 us
  Pallas kernels  20.6 us (93%)
  between operations  0.66 us (3%)
  local copies, waits for them, and re-layouts  0.61 us (3%)
    pallas_call x1, Pallas kernels, on_device(): pl.pallas_call(functools.partial(kernel, n), out_shape=pltpu.VMEM((feat,...  20.6 us
    unnamed x1, local copies, waits for them, and re-layouts  0.61 us

profile of v2, /device:TPU:1, one launch (start us, length us, event | category | flops | bytes accessed | tf_op | source)
XLA Modules:
  0.0 21.9 jit_solution(10491924746270867015)
XLA Ops:
  0.7 20.6 %shard_map.46 = f32[48,128]{1,0:T(8,128)S(1)} custom-call(bf16[48,8192]{1,0:T(8,128)(2,1)} %src_hbm.1, bf16[640,128,128]{2,1,0:T(8,128)(2,1)} %w_hbm.1, s32[3,640]{1,0:T(4,128)} %map_hbm.1, s32[1]{0:T(128)S(6)} %copy.7.cnt_s), custom_call_target="tpu_custom_call" | custom-call | flops 1006632960 | bytes 20971520 | tf_op jit(solution)/shard_map/pallas_call | solution.py:122
  21.3 0.6 %copy.6 = f32[48,128]{1,0:T(8,128)} copy(f32[48,128]{1,0:T(8,128)S(1)} %shard_map.46) | data formatting | bytes 49152

commit v3 on v2

--- a/solution.py
+++ b/solution.py
@@ -12,7 +12,7 @@
 CHUNK = 64
 
 
-def kernel(n, src_hbm, w_hbm, map_hbm, cnt_s, out_ref, w, src, log, map_v, map_s, idx_v, idx_s, send, recv,
+def kernel(n, src_hbm, w_hbm, map_hbm, cnt_s, out_ref, w, src_flat, src, log, map_v, map_s, idx_v, idx_s, send, recv,
            w_sem, in_sem, send_sem, recv_sem):
     tiles, blk = w.shape[0], w.shape[1]
     feat = src.shape[1]
@@ -24,14 +24,11 @@
 
     map_copy = pltpu.make_async_copy(map_hbm, map_v, in_sem.at[0])
     map_copy_s = pltpu.make_async_copy(map_hbm, map_s, in_sem.at[1])
-    src_copy = pltpu.make_async_copy(src, src, in_sem.at[2])
+    src_copy = pltpu.make_async_copy(src_hbm, src_flat, in_sem.at[2])
     map_copy.start()
     map_copy_s.start()
 
-    @pl.loop(0, src.shape[0])
-    def _(b):
-        part = pl.ds(pl.multiple_of(b * blk, blk), blk)
-        pltpu.make_async_copy(src_hbm.at[:, part], src.at[b], in_sem.at[2]).start()
+    src_copy.start()
 
     def w_copy(c):
         part = pl.ds(pl.multiple_of(c * CHUNK, CHUNK), CHUNK)
@@ -63,14 +60,17 @@
             prev = jnp.where(columns[h] == keys[g], row + (h * LANES + 1), prev)
         here = jnp.logical_and(columns[g] == keys[g], row < lane)
         prev = jnp.where(here, row + (g * LANES + 1), prev)
-        idx_v[:, g * LANES:(g + 1) * LANES] = jnp.max(prev, axis=0, keepdims=True)
+        prev = jnp.max(prev, axis=0, keepdims=True)
+        idx_v[:, g * LANES:(g + 1) * LANES] = jnp.where(lane + g * LANES < cnt_s[0], prev, 0)
         last = jnp.where(columns[g] == lane, row + (g * LANES + 1), last)
     idx_v[:, tiles:tiles + LANES] = jnp.max(last, axis=0, keepdims=True)
     idx_copy = pltpu.make_async_copy(idx_v, idx_s, in_sem.at[3])
     idx_copy.start()
     log[0] = jnp.zeros((feat, blk), jnp.float32)
+    src_copy.wait()
+    for b in range(src.shape[0]):
+        src[b] = src_flat[:, b * blk:(b + 1) * blk]
     map_copy_s.wait()
-    src_copy.wait()
     idx_copy.wait()
 
     @pl.loop(0, chunks)
@@ -126,6 +126,7 @@
         out_specs=pl.BlockSpec(memory_space=pltpu.VMEM),
         scratch_shapes=[
             pltpu.VMEM((tiles, blk, blk), jnp.bfloat16),
+            pltpu.VMEM((feat, cells), jnp.bfloat16),
             pltpu.VMEM((cells // blk, feat, blk), jnp.bfloat16),
             pltpu.VMEM((tiles + 1, feat, blk), jnp.float32),
             pltpu.VMEM(tile_map.shape, jnp.int32),

time: 22.1 us -> 21.4 us (0.968)
  Pallas kernels: 20.6 us -> 20 us
    pallas_call x1, Pallas kernels: 20.6 us -> 20 us  [on_device(): pl.pallas_call(functools.partial(kernel, n), out_shape=pltpu.VMEM((feat,...]
where the time goes in v3:
time: 21.4 us; the launch traced here: 21.3 us
  Pallas kernels  20 us (93%)
  between operations  0.66 us (3%)
  local copies, waits for them, and re-layouts  0.61 us (3%)
    pallas_call x1, Pallas kernels, on_device(): pl.pallas_call(functools.partial(kernel, n), out_shape=pltpu.VMEM((feat,...  20 us
    unnamed x1, local copies, waits for them, and re-layouts  0.61 us

profile of v3, /device:TPU:1, one launch (start us, length us, event | category | flops | bytes accessed | tf_op | source)
XLA Modules:
  0.0 21.3 jit_solution(3510478382139874562)
XLA Ops:
  0.7 20.0 %shard_map.46 = f32[48,128]{1,0:T(8,128)S(1)} custom-call(bf16[48,8192]{1,0:T(8,128)(2,1)} %src_hbm.1, bf16[640,128,128]{2,1,0:T(8,128)(2,1)} %w_hbm.1, s32[3,640]{1,0:T(4,128)} %map_hbm.1, s32[1]{0:T(128)S(6)} %copy.7.cnt_s), custom_call_target="tpu_custom_call" | custom-call | flops 1006632960 | bytes 20971520 | tf_op jit(solution)/shard_map/pallas_call | solution.py:122
  20.7 0.6 %copy.6 = f32[48,128]{1,0:T(8,128)} copy(f32[48,128]{1,0:T(8,128)S(1)} %shard_map.46) | data formatting | bytes 49152

commit v4 on v3

--- a/solution.py
+++ b/solution.py
@@ -97,18 +97,25 @@
             device_id=(partner,), device_id_type=pl.DeviceIdType.MESH)
 
     place = lax.rem(own, 4)
-    for turn in range(REACH):
-        step = jnp.where(place == 3, (2, 1, 4, 3)[turn], jnp.where(place == 2, (3, 2, 4, 1)[turn], REACH - turn))
-        transfer(step + (REACH - 1), lax.rem(own + step, n)).start()
+    steps = [jnp.where(place == 3, (2, 1, 4, 3)[turn], jnp.where(place == 2, (3, 2, 4, 1)[turn], REACH - turn))
+             for turn in range(REACH)]
+    transfer(steps[0] + (REACH - 1), lax.rem(own + steps[0], n)).start()
+    transfer(steps[1] + (REACH - 1), lax.rem(own + steps[1], n)).start()
+    transfer(steps[2] + (REACH - 1), lax.rem(own + steps[2], n)).start()
+    transfer(steps[3] + (REACH - 1), lax.rem(own + steps[3], n)).start()
+    transfer(steps[0] + (REACH - 1), lax.rem(own + steps[0], n)).wait_send()
+    transfer(steps[1] + (REACH - 1), lax.rem(own + steps[1], n)).wait_send()
+    transfer(steps[2] + (REACH - 1), lax.rem(own + steps[2], n)).wait_send()
+    transfer(steps[3] + (REACH - 1), lax.rem(own + steps[3], n)).wait_send()
     for k in range(REACH):
         transfer(k, partners[k]).start()
     transfer(2 * REACH, partners[2 * REACH]).start()
     total = log[idx_s[0, tiles + REACH]]
-    for k in range(len(offsets)):
+    for k in list(range(REACH)) + [2 * REACH, REACH, 2 * REACH - 1, REACH + 1, REACH + 2]:
         transfer(k, partners[k]).wait_recv()
         total = total + recv[k]
     out_ref[...] = total
-    for k in range(len(offsets)):
+    for k in list(range(REACH)) + [2 * REACH]:
         transfer(k, partners[k]).wait_send()
 
 

time: 21.4 us -> 21.4 us (level)
  no operation moved by 1% of the time
where the time goes in v4:
time: 21.4 us; the launch traced here: 21.2 us
  Pallas kernels  19.9 us (93%)
  between operations  0.66 us (3%)
  local copies, waits for them, and re-layouts  0.61 us (3%)
    pallas_call x1, Pallas kernels, on_device(): pl.pallas_call(functools.partial(kernel, n), out_shape=pltpu.VMEM((feat,...  19.9 us
    unnamed x1, local copies, waits for them, and re-layouts  0.61 us

profile of v4, /device:TPU:1, one launch (start us, length us, event | category | flops | bytes accessed | tf_op | source)
XLA Modules:
  0.0 21.2 jit_solution(1352691465402705396)
XLA Ops:
  0.7 19.9 %shard_map.46 = f32[48,128]{1,0:T(8,128)S(1)} custom-call(bf16[48,8192]{1,0:T(8,128)(2,1)} %src_hbm.1, bf16[640,128,128]{2,1,0:T(8,128)(2,1)} %w_hbm.1, s32[3,640]{1,0:T(4,128)} %map_hbm.1, s32[1]{0:T(128)S(6)} %copy.7.cnt_s), custom_call_target="tpu_custom_call" | custom-call | flops 1006632960 | bytes 20971520 | tf_op jit(solution)/shard_map/pallas_call | solution.py:129
  20.6 0.6 %copy.6 = f32[48,128]{1,0:T(8,128)} copy(f32[48,128]{1,0:T(8,128)S(1)} %shard_map.46) | data formatting | bytes 49152
